TPU v7x, 32 devices: a whole 2x2x4 slice. The times are simulated.
32 devices in a mesh: row: 4 (over x, core), col: 4 (over z), layer: 2 (over y).
Axes of the slice: x: 2, y: 2, z: 4, core: 2. Of those that a mesh axis runs over, the one named last changes fastest.
Arguments:
- left_factor: float32 [6144, 8192], P('row', 'col'), may hold values from -6 to 6
- right_factor: float32 [8192, 6144], P('row', 'col'), may hold values from -0.0625 to 0.0625
Outputs:
- product: float32 [6144, 6144], P(('row', 'layer'), 'col')
All inputs are finite; a program needn't handle non-finite values.
Results may differ from a plain program's by a relative error of at most 0.000073.
Values sent between devices are 32-bit elements; how exact they have to be, the bound alone decides.
A program may use at most 192 MiB of HBM per device.

v0:
```python
import jax
import jax.numpy as jnp
from jax import lax
from jax.experimental import pallas as pl
from jax.experimental.pallas import tpu as pltpu
from jax.sharding import PartitionSpec as P

MESH = pl.DeviceIdType.MESH
EVEN = (1, 1, 1, 1)
PARTS = (4, 4, 4, 2, 2)
LANES = 512
PIECES = 8
SUBS = ((0, 2), (0, 3), (0, 0), (1, 0), (0, 1), (1, 1))


def product(left, right):
    return jnp.dot(
        left,
        right,
        precision=lax.Precision.HIGH,
        preferred_element_type=jnp.float32,
    )


def gathered(left_factor, right_factor):
    layers = lax.axis_size("layer")
    rows = left_factor.shape[0] // layers
    left = lax.dynamic_slice_in_dim(left_factor, lax.axis_index("layer") * rows, rows, 0)
    left = lax.all_gather(left, "col", axis=1, tiled=True)
    right = lax.all_gather(right_factor, "row", axis=0, tiled=True)
    return product(left, right)


def keys():
    n, table = 0, {}
    counts = dict(AE=len(PARTS), AB=len(EVEN), AO=len(EVEN), AF=len(PARTS), CX=len(PARTS))
    counts.update(X=len(SUBS), XE=len(SUBS), MC=2, MX=PIECES, MY=PIECES, MF=2 * PIECES)
    counts.update(PX=len(SUBS), PO=2, PF=2, C0=len(SUBS), C1=len(SUBS), C2=2, C3=2)
    for name, count in counts.items():
        for i in range(count):
            table[name, i] = n
            n += 1
    return table


KEYS = keys()


def kernel(left, right, out, abuf, bmain, bx, acc, exacc, atile, btile, ftile, send, recv, asem, bsem, osem):
    row, z, layer = (lax.axis_index(name) for name in ("row", "col", "layer"))
    rows, wide = acc.shape
    depth = right.shape[0]
    half = depth // 2
    tall = rows // len(EVEN)
    core = lax.rem(row, 2)
    low = z < 2
    edge = (z == 0) | (z == 3)
    near = (row // 2) == (z // 2)
    farther = jnp.where(near, 0, 1)
    row_x = lax.rem(row + 2, 4)
    row_c = row + 1 - 2 * core
    outer = jnp.where(low, z - 1, z + 1)
    inner = jnp.where(low, z + 1, z - 1)
    flip = 1 - layer
    by_x, by_c, by_y = {"row": row_x}, {"row": row_c}, {"layer": flip}
    by_out, by_in = {"col": outer}, {"col": inner}
    my_rows = layer * rows

    def remote(src, dst, key, device):
        k = KEYS[key]
        return pltpu.make_async_remote_copy(
            src_ref=src, dst_ref=dst, send_sem=send.at[k], recv_sem=recv.at[k], device_id=device, device_id_type=MESH
        )

    sent = []

    def put(src, dst, key, device):
        remote(src, dst, key, device).start()
        if (src.shape, key) not in sent:
            sent.append((src.shape, key))

    def got(dst, key):
        remote(dst, dst, key, by_c).wait_recv()

    def span(parts, i):
        size = rows // sum(parts)
        return sum(parts[:i]) * size, parts[i] * size

    def own_a(parts, i):
        start, size = span(parts, i)
        return left.at[pl.ds(my_rows + start, size), :]

    def slot_a(slot, parts, i):
        start, size = span(parts, i)
        return abuf.at[slot, pl.ds(start, size), :]

    def aligned(value):
        return pl.multiple_of(value, 128)

    cut = half // PIECES
    sub = half // 8

    def main(slot, which, p):
        return bmain.at[slot, pl.ds(aligned(which * half + p * cut), cut), :]

    def mine(p):
        return right.at[pl.ds(aligned(layer * half + p * cut), cut), :]

    def extra(q, far, which, t):
        return bx.at[q, pl.ds(aligned(which * half + far * (half // 2) + t * sub), sub), :]

    def extra_source(ref, far, k):
        other, t = SUBS[k]
        which = flip if other else layer
        return ref.at[pl.ds(aligned(which * half + far * (half // 2) + t * sub), sub), :]

    def extra_place(q, far, k):
        other, t = SUBS[k]
        return extra(q, far, flip if other else layer, t)

    spot = jnp.where(near, 1, 0)

    def load_a(view, sem, block, start, col):
        size, deep = view.shape
        where = pl.ds(aligned(col), deep)
        own = block == z
        turned = jnp.where(low, block, 3 - block)
        slot = jnp.maximum(turned - 1, 0)

        @pl.when(own)
        def _():
            pltpu.make_async_copy(left.at[pl.ds(my_rows + start, size), where], view, sem).start()

        @pl.when(jnp.logical_not(own))
        def _():
            pltpu.make_async_copy(abuf.at[slot, pl.ds(start, size), where], view, sem).start()

    def load_b(view, sem, term, first):
        where = pl.ds(aligned(first), view.shape[0])

        @pl.when(term == 0)
        def _():
            pltpu.make_async_copy(right.at[where, :], view, sem).start()

        @pl.when(term > 0)
        def _():
            pltpu.make_async_copy(bmain.at[jnp.maximum(term - 1, 0), where, :], view, sem).start()

    def landed(view, sem):
        pltpu.make_async_copy(view, view, sem).wait()

    def owner(term):
        return jnp.where(term == 0, row, jnp.where(term == 1, row_c, jnp.where(term == 2, row_x, 3 - row)))

    def multiply(total, start, lhs, weights):
        size = lhs.shape[0]

        def lanes(t, carry):
            columns = pl.ds(pl.multiple_of(t * LANES, LANES), LANES)
            total[pl.ds(start, size), columns] += product(lhs[...], weights(columns))
            return carry

        lax.fori_loop(0, wide // LANES, lanes, 0)

    def play(plan):
        runs, first = [], []
        for kind, *what in plan:
            if kind == "run":
                runs.append((what, [], []))
            elif not runs:
                first.append(what[0])
            else:
                runs[-1][1 if kind == "do" else 2].append(what[0])
        for act in first:
            act()
        base = 0
        for index, ((count, load, use), acts, after) in enumerate(runs):
            if index == 0:
                load(0, 0)
            following = runs[index + 1][0][1] if index + 1 < len(runs) else None

            def step(j, carry, count=count, load=load, use=use, acts=acts, following=following, base=base):
                slot = lax.rem(j + base, 2)

                @pl.when(j + 1 < count)
                def _():
                    load(j + 1, 1 - slot)

                @pl.when(j + 1 == count)
                def _():
                    for act in acts:
                        act()
                    if following is not None:
                        following(0, 1 - slot)

                use(j, slot)
                return carry

            lax.fori_loop(0, count, step, 0)
            for act in after:
                act()
            base = (base + count) % 2

    def own_jobs(count, job):
        def load(j, slot):
            term, first, start = job(j)
            load_a(atile.at[slot], asem.at[slot], owner(term), start, first)
            load_b(btile.at[slot], bsem.at[slot], term, first)

        def use(j, slot):
            landed(atile.at[slot], asem.at[slot])
            landed(btile.at[slot], bsem.at[slot])
            start = pl.multiple_of(job(j)[2], 8)
            multiply(acc, start, atile.at[slot], lambda columns: btile[slot, :, columns])

        return ("run", count, load, use)

    def far_jobs(count, job):
        deep = half // 2

        def load(j, slot):
            term, first, start = job(j)
            load_a(ftile.at[slot], asem.at[slot], owner(term), start, first)
            load_b(btile.at[slot, pl.ds(0, deep), :], bsem.at[slot], term, first)

        def use(j, slot):
            landed(ftile.at[slot], asem.at[slot])
            landed(btile.at[slot, pl.ds(0, deep), :], bsem.at[slot])
            start = pl.multiple_of(job(j)[2], 8)
            multiply(acc, start, ftile.at[slot], lambda columns: btile[slot, pl.ds(0, deep), columns])

        return ("run", count, load, use)

    def extra_jobs(count, size, job):
        def view(slot):
            return atile.at[slot, pl.ds(0, size), :]

        def load(j, slot):
            which, part, start = job(j)
            block = jnp.where(low, 2 + which, 1 - which)
            load_a(view(slot), asem.at[slot], block, start, part * half)

        def use(j, slot):
            which, part, start = job(j)
            landed(view(slot), asem.at[slot])
            q = jnp.where(low, which, 1 - which)
            first = aligned(part * half)
            multiply(exacc, pl.multiple_of(start, 8), view(slot), lambda columns: bx[q, pl.ds(first, half), columns])

        return ("run", count, load, use)

    def write(start, size, k):
        copy = pltpu.make_async_copy(acc.at[pl.ds(start, size), :], out.at[pl.ds(start, size), :], osem.at[k])
        copy.start()
        return copy

    chunks = range(len(PARTS))
    evens = range(len(EVEN))
    barrier = pltpu.get_barrier_semaphore()
    for device in (by_c, by_x, by_y, by_in):
        pl.semaphore_signal(barrier, inc=1, device_id=device, device_id_type=MESH)

    @pl.when(jnp.logical_not(edge))
    def _():
        pl.semaphore_signal(barrier, inc=1, device_id=by_out, device_id_type=MESH)

    pl.semaphore_wait(barrier, jnp.where(edge, 4, 5))

    def drain():
        for (high, broad), key in sent:
            view = (right if broad == wide else left).at[pl.ds(0, high), pl.ds(0, broad)]
            remote(view, view, key, by_c).wait_send()
        sent.clear()

    def edge_end():
        for i in evens:
            got(slot_a(0, EVEN, i), ("AB", i))
        count = len(EVEN)
        play([own_jobs(4 * count, lambda j: (2 * farther + j // (2 * count), lax.rem(j // count, 2) * half, lax.rem(j, count) * tall))])
        copies = []
        for i in chunks:
            start, size = span(PARTS, i)
            view = exacc.at[pl.ds(start, size), :]
            got(view, ("CX", i))
            acc[pl.ds(start, size), :] += view[...]
            copies.append(write(start, size, i))
        for copy in copies:
            copy.wait()
        drain()

    @pl.when(edge & near)
    def _():
        put(own_a(PARTS, 0), slot_a(0, PARTS, 0), ("AE", 0), by_in)
        for p in range(PIECES):
            put(mine(p), main(1, layer, p), ("MX", p), by_x)
        for h in range(2):
            put(right.at[pl.ds(h * half, half), :], bmain.at[0, pl.ds(h * half, half), :], ("MC", h), by_c)
        acc[...] = jnp.zeros_like(acc)
        for k in range(len(SUBS)):
            got(extra_source(bmain.at[1], 1, k), ("XE", k))
            put(extra_source(bmain.at[1], 1, k), extra_place(core, 1, k), ("X", k), by_in)
        for i in chunks[1:]:
            put(own_a(PARTS, i), slot_a(0, PARTS, i), ("AE", i), by_in)
        for h in range(2):
            got(bmain.at[0, pl.ds(h * half, half), :], ("MC", h))
        edge_end()

    @pl.when(edge & jnp.logical_not(near))
    def _():
        for k in range(len(SUBS)):
            if k == 4:
                put(own_a(PARTS, 0), slot_a(0, PARTS, 0), ("AE", 0), by_in)
            put(extra_source(right, 0, k), extra_place(core, 0, k), ("X", k), by_in)
            put(extra_source(right, 1, k), extra_source(bmain.at[1], 1, k), ("XE", k), by_x)
        for i in chunks[1:]:
            put(own_a(PARTS, i), slot_a(0, PARTS, i), ("AE", i), by_in)
        acc[...] = jnp.zeros_like(acc)
        for p in range(PIECES):
            got(main(1, layer, p), ("MX", p))
            put(main(1, layer, p), main(1, layer, p), ("MY", p), by_y)
            put(main(1, layer, p), main(2, layer, p), ("MF", p), by_c)
        for p in range(PIECES):
            got(main(1, flip, p), ("MY", p))
            put(main(1, flip, p), main(2, flip, p), ("MF", PIECES + p), by_c)
        for p in range(PIECES):
            got(main(2, layer, p), ("MF", p))
            got(main(2, flip, p), ("MF", PIECES + p))
        edge_end()

    @pl.when(jnp.logical_not(edge))
    def _():
        inner_term = jnp.where((row == 1) | (row == 2), 0, 1)
        outer_term = 1 - inner_term
        inner_far = 3 - inner_term
        outer_far = 2 + inner_term

        def from_outer(k):
            other, t = SUBS[k]
            view = extra_place(core, spot, k)
            got(view, ("X", k))
            put(view, view, ("PX", k), by_x)
            put(view, view, ("C0", k), by_c)
            if not other and t >= 2:
                put(view, view, ("PO", t - 2), by_y)

        def from_x(k):
            other, t = SUBS[k]
            view = extra_place(core, 1 - spot, k)
            got(view, ("PX", k))
            put(view, view, ("C1", k), by_c)
            if not other and t >= 2:
                put(view, view, ("PF", t - 2), by_y)

        def from_y(i):
            view = extra(core, spot, flip, i + 2)
            got(view, ("PO", i))
            put(view, view, ("C2", i), by_c)

        def across_y(i):
            view = extra(core, 1 - spot, flip, i + 2)
            got(view, ("PF", i))
            put(view, view, ("C3", i), by_c)

        def ahead(i):
            got(slot_a(0, PARTS, i), ("AE", i))
            put(slot_a(0, PARTS, i), slot_a(2, PARTS, i), ("AF", i), by_in)

        def take_x(p):
            got(main(1, layer, p), ("MX", p))
            put(main(1, layer, p), main(1, layer, p), ("MY", p), by_y)
            put(main(1, layer, p), main(2, layer, p), ("MF", p), by_c)

        def take_y(p):
            got(main(1, flip, p), ("MY", p))
            put(main(1, flip, p), main(2, flip, p), ("MF", PIECES + p), by_c)

        def inner_arrived(i):
            got(slot_a(1, EVEN, i), ("AO", i))

        def outer_arrived(i):
            got(slot_a(2, PARTS, i), ("AF", i))

        def inner_units(i):
            return own_jobs(2, lambda j: (inner_term, j * half, i * tall))

        def outer_units(i):
            return own_jobs(2, lambda j: (outer_term, j * half, i * tall))

        def far_units(terms, quarters, pairs):
            jobs = [(t, q, r) for t in terms for q in quarters for r in pairs]

            def pick(j, values):
                value = values[-1]
                for k in range(len(values) - 1):
                    value = jnp.where(j == k, values[k], value)
                return value

            firsts = [jnp.where(layer == (0 if q < 2 else 1), 0, 1) * half + (q % 2) * (half // 2) for q in range(4)]
            return far_jobs(
                len(jobs),
                lambda j: (
                    pick(j, [t for t, _, _ in jobs]),
                    pick(j, [firsts[q] for _, q, _ in jobs]),
                    pick(j, [r * 2 * tall for _, _, r in jobs]),
                ),
            )

        def send_sum(i):
            start, size = span(PARTS, i)
            put(exacc.at[pl.ds(start, size), :], exacc.at[pl.ds(start, size), :], ("CX", i), by_out)

        def outer_extra(i):
            start, size = span(PARTS, i)
            return extra_jobs(2, size, lambda j: (1, j, start))

        for h in range(2):
            put(right.at[pl.ds(h * half, half), :], bmain.at[0, pl.ds(h * half, half), :], ("MC", h), by_c)
        for i in evens:
            put(own_a(EVEN, i), slot_a(1, EVEN, i), ("AO", i), by_in)
        def give(p):
            put(mine(p), main(1, layer, p), ("MX", p), by_x)

        for p in range(2):
            give(p)
        for i in evens:
            put(own_a(EVEN, i), slot_a(0, EVEN, i), ("AB", i), by_out)
        exacc[...] = jnp.zeros_like(exacc)
        acc[...] = jnp.zeros_like(acc)

        def own_whole():
            for h in range(2):
                got(bmain.at[0, pl.ds(h * half, half), :], ("MC", h))

        def extras_whole():
            twin = 1 - core
            for k in range(len(SUBS)):
                got(extra_place(twin, spot, k), ("C0", k))
                got(extra_place(twin, 1 - spot, k), ("C1", k))
            for i in range(2):
                got(extra(twin, spot, flip, i + 2), ("C2", i))
                got(extra(twin, 1 - spot, flip, i + 2), ("C3", i))

        def whole(quarter):
            which, first = (layer, 0) if quarter < 2 else (flip, PIECES)
            for p in range(PIECES // 2 * (quarter % 2), PIECES // 2 * (quarter % 2 + 1)):
                got(main(2, which, p), ("MF", first + p))

        plan = []

        def do(act, *args):
            plan.append(("do", lambda: act(*args)))

        def then(act, *args):
            plan.append(("then", lambda: act(*args)))

        def only(side, acts):
            def act():
                @pl.when(near if side == "near" else jnp.logical_not(near))
                def _():
                    for what, *args in acts:
                        what(*args)

            plan.append(("do", act))

        only("far", [(from_outer, 0)])
        do(take_x, 0)
        do(take_x, 1)
        only("far", [(from_outer, 1)])
        only("near", [(give, 2)])
        do(own_whole)
        do(inner_arrived, 0)
        plan.append(inner_units(0))
        only("far", [(from_outer, 2), (from_outer, 3), (give, 2), (from_x, 0)])
        only("near", [(from_outer, 0), (from_x, 0), (from_outer, 1), (from_x, 1)])
        do(inner_arrived, 1)
        plan.append(inner_units(1))
        only("far", [(take_x, 2), (from_x, 1), (from_y, 0), (from_x, 2)])
        only("near", [(from_outer, 2), (from_x, 2), (from_y, 0), (from_outer, 3), (from_x, 3)])
        do(ahead, 0)
        do(inner_arrived, 2)
        plan.append(inner_units(2))
        do(from_y, 1)
        do(across_y, 0)
        do(from_outer, 4)
        only("far", [(from_x, 3)])
        only("near", [(take_x, 2)])
        do(across_y, 1)
        do(from_outer, 5)
        for p in range(3, PIECES):
            do(give, p)
        do(inner_arrived, 3)
        plan.append(inner_units(3))
        do(from_x, 4)
        do(from_x, 5)
        do(extras_whole)
        plan.append(extra_jobs(4, tall, lambda j: (0, lax.rem(j, 2), (j // 2) * tall)))
        do(ahead, 1)
        plan.append(extra_jobs(4, tall, lambda j: (0, lax.rem(j, 2), (2 + j // 2) * tall)))
        do(outer_arrived, 0)
        plan.append(outer_extra(0))
        then(send_sum, 0)
        do(take_x, 3)
        plan.append(outer_units(0))
        do(whole, 0)
        plan.append(far_units([inner_far], [0], [0, 1]))
        do(ahead, 2)
        do(take_x, 4)
        do(outer_arrived, 1)
        plan.append(outer_extra(1))
        then(send_sum, 1)
        plan.append(outer_units(1))
        for p in range(4):
            do(take_y, p)
        do(take_x, 5)
        do(whole, 2)
        plan.append(far_units([inner_far], [2], [0, 1]))
        plan.append(far_units([outer_far], [0, 2], [0]))
        do(take_x, 6)
        for i in chunks[3:]:
            do(ahead, i)
        do(outer_arrived, 2)
        plan.append(outer_extra(2))
        then(send_sum, 2)
        do(take_x, 7)
        plan.append(outer_units(2))
        do(whole, 1)
        plan.append(far_units([inner_far], [1], [0, 1]))
        do(outer_arrived, 3)
        plan.append(far_units([outer_far], [1], [0]))
        plan.append(outer_extra(3))
        then(send_sum, 3)
        plan.append(own_jobs(1, lambda j: (outer_far, layer * half, 2 * tall)))
        for p in range(4, PIECES):
            do(take_y, p)
        do(whole, 3)
        plan.append(far_units([inner_far], [3], [0, 1]))
        do(outer_arrived, 4)
        plan.append(far_units([outer_far], [3], [0]))
        then(write, 0, 2 * tall, 0)
        plan.append(outer_extra(4))
        then(send_sum, 4)
        plan.append(own_jobs(1, lambda j: (outer_far, flip * half, 2 * tall)))
        plan.append(outer_units(3))
        plan.append(own_jobs(2, lambda j: (outer_far, j * half, 3 * tall)))
        play(plan)
        write(2 * tall, 2 * tall, 1)
        for k in range(2):
            view = acc.at[pl.ds(0, 2 * tall), :]
            pltpu.make_async_copy(view, view, osem.at[k]).wait()
        drain()


def line(left_factor, right_factor):
    depth, wide = right_factor.shape
    rows = left_factor.shape[0] // 2
    tall = rows // len(EVEN)
    half = depth // 2
    any_space = pl.BlockSpec(memory_space=pl.ANY)
    copies = len(KEYS)
    f32 = jnp.float32
    return pl.pallas_call(
        kernel,
        out_shape=(
            jax.ShapeDtypeStruct((rows, wide), f32),
            jax.ShapeDtypeStruct((3, rows, depth), f32),
            jax.ShapeDtypeStruct((3, depth, wide), f32),
        ),
        in_specs=[any_space] * 2,
        out_specs=[any_space] * 3,
        scratch_shapes=[
            pltpu.VMEM((2, depth, wide), f32),
            pltpu.VMEM((rows, wide), f32),
            pltpu.VMEM((rows, wide), f32),
            pltpu.VMEM((2, tall, half), f32),
            pltpu.VMEM((2, half, wide), f32),
            pltpu.VMEM((2, 2 * tall, half // 2), f32),
            pltpu.SemaphoreType.DMA((copies,)),
            pltpu.SemaphoreType.DMA((copies,)),
            pltpu.SemaphoreType.DMA((2,)),
            pltpu.SemaphoreType.DMA((2,)),
            pltpu.SemaphoreType.DMA((len(PARTS),)),
        ],
        compiler_params=pltpu.CompilerParams(collective_id=0, has_side_effects=True, vmem_limit_bytes=67043328),
        name="line",
    )(left_factor, right_factor)[0]


def solution(mesh):
    placed = (P("row", "col"), P("row", "col"))
    fits = (mesh.shape["row"], mesh.shape["col"], mesh.shape["layer"]) == (4, 4, 2)
    return jax.shard_map(
        line if fits else gathered,
        mesh=mesh,
        in_specs=placed,
        out_specs=P(("row", "layer"), "col"),
        check_vma=False,
    )
```

profile of v0, /device:TPU:15, one launch (start us, length us, event | category | flops | bytes accessed | tf_op | source)
XLA Modules:
  0.0 313.0 jit_solution(15644441939856793724)
XLA Ops:
  0.0 308.1 %line.1 = (f32[768,1536]{1,0:T(8,128)}, f32[3,768,2048]{2,1,0:T(8,128)}, f32[3,2048,1536]{2,1,0:T(8,128)}) custom-call(f32[1536,2048]{1,0:T(8,128)} %left.1, f32[2048,1536]{1,0:T(8,128)} %right.1), custom_call_target="tpu_custom_call" | custom-call | tf_op jit(solution)/shard_map/line/pallas_call | solution.py:561
  308.1 4.8 %copy.4 = f32[768,1536]{1,0:T(8,128)} copy(f32[768,1536]{1,0:T(8,128)} %get-tuple-element.6) | data formatting | bytes 9437184
where the time goes:
time: 315 us; the launch traced here: 313 us
  Pallas kernels  308 us (98%)
  local copies, waits for them, and re-layouts  4.84 us (2%)
    pallas_call x1, Pallas kernels, line(): pl.pallas_call(kernel, out_shape=(jax.ShapeDtypeStruct((rows, wide), f32)...  308 us

commit v1 on v0

--- a/solution.py
+++ b/solution.py
@@ -8,7 +8,9 @@
 MESH = pl.DeviceIdType.MESH
 EVEN = (1, 1, 1, 1)
 PARTS = (4, 4, 4, 2, 2)
+OUTER = ((0, None), (1, None), (2, 0), (2, 1), (3, None), (4, 0), (4, 1))
 LANES = 512
+LAST = 3
 PIECES = 8
 SUBS = ((0, 2), (0, 3), (0, 0), (1, 0), (0, 1), (1, 1))
 
@@ -33,7 +35,7 @@
 
 def keys():
     n, table = 0, {}
-    counts = dict(AE=len(PARTS), AB=len(EVEN), AO=len(EVEN), AF=len(PARTS), CX=len(PARTS))
+    counts = dict(AE=len(OUTER), AB=len(EVEN), AO=len(EVEN), AF=len(OUTER), CX=len(PARTS) + LAST - 1)
     counts.update(X=len(SUBS), XE=len(SUBS), MC=2, MX=PIECES, MY=PIECES, MF=2 * PIECES)
     counts.update(PX=len(SUBS), PO=2, PF=2, C0=len(SUBS), C1=len(SUBS), C2=2, C3=2)
     for name, count in counts.items():
@@ -46,7 +48,20 @@
 KEYS = keys()
 
 
-def kernel(left, right, out, abuf, bmain, bx, acc, exacc, atile, btile, ftile, send, recv, asem, bsem, osem):
+def sums(rows, wide):
+    unit = rows // sum(PARTS)
+    pieces = []
+    for i, part in enumerate(PARTS):
+        start = sum(PARTS[:i]) * unit
+        if i < len(PARTS) - 1:
+            pieces.append((("CX", i), start, part * unit, 0, wide))
+        else:
+            lanes = wide // LAST
+            pieces += [(("CX", i + t), start, part * unit, t * lanes, lanes) for t in range(LAST)]
+    return pieces
+
+
+def kernel(left, right, acc, abuf, bmain, bx, exacc, atile, btile, ftile, send, recv, asem, bsem):
     row, z, layer = (lax.axis_index(name) for name in ("row", "col", "layer"))
     rows, wide = acc.shape
     depth = right.shape[0]
@@ -94,6 +109,15 @@
         start, size = span(parts, i)
         return abuf.at[slot, pl.ds(start, size), :]
 
+    def side(part):
+        return lax.rem(layer + part, 2)
+
+    def piece(ref, offset, k):
+        i, part = OUTER[k]
+        start, size = span(PARTS, i)
+        where = pl.ds(0, depth) if part is None else pl.ds(aligned(side(part) * half), half)
+        return ref.at[pl.ds(offset + start, size), where]
+
     def aligned(value):
         return pl.multiple_of(value, 128)
 
@@ -231,28 +255,28 @@
 
         return ("run", count, load, use)
 
-    def extra_jobs(count, size, job):
+    def extra_jobs(count, size, job, pieces=()):
         def view(slot):
             return atile.at[slot, pl.ds(0, size), :]
 
         def load(j, slot):
             which, part, start = job(j)
             block = jnp.where(low, 2 + which, 1 - which)
-            load_a(view(slot), asem.at[slot], block, start, part * half)
+            load_a(view(slot), asem.at[slot], block, start, side(part) * half)
 
         def use(j, slot):
             which, part, start = job(j)
             landed(view(slot), asem.at[slot])
             q = jnp.where(low, which, 1 - which)
-            first = aligned(part * half)
-            multiply(exacc, pl.multiple_of(start, 8), view(slot), lambda columns: bx[q, pl.ds(first, half), columns])
+            first = aligned(side(part) * half)
+            if not pieces:
+                multiply(exacc, pl.multiple_of(start, 8), view(slot), lambda columns: bx[q, pl.ds(first, half), columns])
+            for key, top, high, begin, broad in pieces:
+                where = (pl.ds(top, high), pl.ds(begin, broad))
+                exacc[where] += product(view(slot)[...], bx[q, pl.ds(first, half), pl.ds(begin, broad)])
+                put(exacc.at[where], exacc.at[where], key, by_out)
 
         return ("run", count, load, use)
-
-    def write(start, size, k):
-        copy = pltpu.make_async_copy(acc.at[pl.ds(start, size), :], out.at[pl.ds(start, size), :], osem.at[k])
-        copy.start()
-        return copy
 
     chunks = range(len(PARTS))
     evens = range(len(EVEN))
@@ -277,20 +301,15 @@
             got(slot_a(0, EVEN, i), ("AB", i))
         count = len(EVEN)
         play([own_jobs(4 * count, lambda j: (2 * farther + j // (2 * count), lax.rem(j // count, 2) * half, lax.rem(j, count) * tall))])
-        copies = []
-        for i in chunks:
-            start, size = span(PARTS, i)
-            view = exacc.at[pl.ds(start, size), :]
-            got(view, ("CX", i))
-            acc[pl.ds(start, size), :] += view[...]
-            copies.append(write(start, size, i))
-        for copy in copies:
-            copy.wait()
+        for key, start, size, first, broad in sums(rows, wide):
+            where = (pl.ds(start, size), pl.ds(first, broad))
+            got(exacc.at[where], key)
+            acc[where] += exacc[where]
         drain()
 
     @pl.when(edge & near)
     def _():
-        put(own_a(PARTS, 0), slot_a(0, PARTS, 0), ("AE", 0), by_in)
+        put(piece(left, my_rows, 0), piece(abuf.at[0], 0, 0), ("AE", 0), by_in)
         for p in range(PIECES):
             put(mine(p), main(1, layer, p), ("MX", p), by_x)
         for h in range(2):
@@ -299,8 +318,8 @@
         for k in range(len(SUBS)):
             got(extra_source(bmain.at[1], 1, k), ("XE", k))
             put(extra_source(bmain.at[1], 1, k), extra_place(core, 1, k), ("X", k), by_in)
-        for i in chunks[1:]:
-            put(own_a(PARTS, i), slot_a(0, PARTS, i), ("AE", i), by_in)
+        for k in range(1, len(OUTER)):
+            put(piece(left, my_rows, k), piece(abuf.at[0], 0, k), ("AE", k), by_in)
         for h in range(2):
             got(bmain.at[0, pl.ds(h * half, half), :], ("MC", h))
         edge_end()
@@ -309,11 +328,11 @@
     def _():
         for k in range(len(SUBS)):
             if k == 4:
-                put(own_a(PARTS, 0), slot_a(0, PARTS, 0), ("AE", 0), by_in)
+                put(piece(left, my_rows, 0), piece(abuf.at[0], 0, 0), ("AE", 0), by_in)
             put(extra_source(right, 0, k), extra_place(core, 0, k), ("X", k), by_in)
             put(extra_source(right, 1, k), extra_source(bmain.at[1], 1, k), ("XE", k), by_x)
-        for i in chunks[1:]:
-            put(own_a(PARTS, i), slot_a(0, PARTS, i), ("AE", i), by_in)
+        for k in range(1, len(OUTER)):
+            put(piece(left, my_rows, k), piece(abuf.at[0], 0, k), ("AE", k), by_in)
         acc[...] = jnp.zeros_like(acc)
         for p in range(PIECES):
             got(main(1, layer, p), ("MX", p))
@@ -361,9 +380,9 @@
             got(view, ("PF", i))
             put(view, view, ("C3", i), by_c)
 
-        def ahead(i):
-            got(slot_a(0, PARTS, i), ("AE", i))
-            put(slot_a(0, PARTS, i), slot_a(2, PARTS, i), ("AF", i), by_in)
+        def ahead(k):
+            got(piece(abuf.at[0], 0, k), ("AE", k))
+            put(piece(abuf.at[0], 0, k), piece(abuf.at[2], 0, k), ("AF", k), by_in)
 
         def take_x(p):
             got(main(1, layer, p), ("MX", p))
@@ -377,24 +396,25 @@
         def inner_arrived(i):
             got(slot_a(1, EVEN, i), ("AO", i))
 
-        def outer_arrived(i):
-            got(slot_a(2, PARTS, i), ("AF", i))
+        def outer_arrived(k):
+            got(piece(abuf.at[2], 0, k), ("AF", k))
 
         def inner_units(i):
             return own_jobs(2, lambda j: (inner_term, j * half, i * tall))
 
-        def outer_units(i):
-            return own_jobs(2, lambda j: (outer_term, j * half, i * tall))
+        def outer_units(i, parts=(0, 1)):
+            return own_jobs(len(parts), lambda j: (outer_term, side(parts[0] + j) * half, i * tall))
+
+        def pick(j, values):
+            value = values[-1]
+            for k in range(len(values) - 1):
+                value = jnp.where(j == k, values[k], value)
+            return value
 
         def far_units(terms, quarters, pairs):
-            jobs = [(t, q, r) for t in terms for q in quarters for r in pairs]
-
-            def pick(j, values):
-                value = values[-1]
-                for k in range(len(values) - 1):
-                    value = jnp.where(j == k, values[k], value)
-                return value
-
+            return far_list([(t, q, r) for t in terms for q in quarters for r in pairs])
+
+        def far_list(jobs):
             firsts = [jnp.where(layer == (0 if q < 2 else 1), 0, 1) * half + (q % 2) * (half // 2) for q in range(4)]
             return far_jobs(
                 len(jobs),
@@ -409,9 +429,10 @@
             start, size = span(PARTS, i)
             put(exacc.at[pl.ds(start, size), :], exacc.at[pl.ds(start, size), :], ("CX", i), by_out)
 
-        def outer_extra(i):
+        def outer_extra(i, parts=(0, 1)):
             start, size = span(PARTS, i)
-            return extra_jobs(2, size, lambda j: (1, j, start))
+            last = [piece for piece in sums(rows, wide) if piece[1] == start] if i == len(PARTS) - 1 and 1 in parts else ()
+            return extra_jobs(len(parts), size, lambda j: (1, parts[0] + j, start), last)
 
         for h in range(2):
             put(right.at[pl.ds(h * half, half), :], bmain.at[0, pl.ds(h * half, half), :], ("MC", h), by_c)
@@ -500,11 +521,12 @@
         plan.append(outer_extra(0))
         then(send_sum, 0)
         do(take_x, 3)
+        do(ahead, 2)
         plan.append(outer_units(0))
         do(whole, 0)
         plan.append(far_units([inner_far], [0], [0, 1]))
-        do(ahead, 2)
         do(take_x, 4)
+        do(ahead, 3)
         do(outer_arrived, 1)
         plan.append(outer_extra(1))
         then(send_sum, 1)
@@ -514,39 +536,39 @@
         do(take_x, 5)
         do(whole, 2)
         plan.append(far_units([inner_far], [2], [0, 1]))
+        do(ahead, 4)
         plan.append(far_units([outer_far], [0, 2], [0]))
         do(take_x, 6)
-        for i in chunks[3:]:
-            do(ahead, i)
         do(outer_arrived, 2)
-        plan.append(outer_extra(2))
+        plan.append(outer_extra(2, (0,)))
+        do(ahead, 5)
+        plan.append(outer_units(2, (0,)))
+        do(ahead, 6)
+        do(outer_arrived, 3)
+        plan.append(outer_extra(2, (1,)))
         then(send_sum, 2)
+        plan.append(outer_units(2, (1,)))
         do(take_x, 7)
-        plan.append(outer_units(2))
+        do(take_y, 4)
         do(whole, 1)
         plan.append(far_units([inner_far], [1], [0, 1]))
-        do(outer_arrived, 3)
         plan.append(far_units([outer_far], [1], [0]))
+        plan.append(own_jobs(1, lambda j: (outer_far, layer * half, 2 * tall)))
+        do(take_y, 5)
+        do(outer_arrived, 4)
         plan.append(outer_extra(3))
         then(send_sum, 3)
-        plan.append(own_jobs(1, lambda j: (outer_far, layer * half, 2 * tall)))
-        for p in range(4, PIECES):
-            do(take_y, p)
+        do(take_y, 6)
+        do(outer_arrived, 5)
+        plan.append(outer_extra(4, (0,)))
+        plan.append(own_jobs(2, lambda j: (jnp.where(j == 0, outer_term, outer_far), layer * half, 3 * tall)))
+        do(take_y, 7)
+        do(outer_arrived, 6)
+        plan.append(outer_extra(4, (1,)))
         do(whole, 3)
-        plan.append(far_units([inner_far], [3], [0, 1]))
-        do(outer_arrived, 4)
-        plan.append(far_units([outer_far], [3], [0]))
-        then(write, 0, 2 * tall, 0)
-        plan.append(outer_extra(4))
-        then(send_sum, 4)
-        plan.append(own_jobs(1, lambda j: (outer_far, flip * half, 2 * tall)))
-        plan.append(outer_units(3))
-        plan.append(own_jobs(2, lambda j: (outer_far, j * half, 3 * tall)))
+        plan.append(far_list([(inner_far, 3, 0), (inner_far, 3, 1), (outer_far, 3, 0), (outer_far, 2, 1), (outer_far, 3, 1)]))
+        plan.append(outer_units(3, (1,)))
         play(plan)
-        write(2 * tall, 2 * tall, 1)
-        for k in range(2):
-            view = acc.at[pl.ds(0, 2 * tall), :]
-            pltpu.make_async_copy(view, view, osem.at[k]).wait()
         drain()
 
 
@@ -561,15 +583,14 @@
     return pl.pallas_call(
         kernel,
         out_shape=(
-            jax.ShapeDtypeStruct((rows, wide), f32),
+            pltpu.VMEM((rows, wide), f32),
             jax.ShapeDtypeStruct((3, rows, depth), f32),
             jax.ShapeDtypeStruct((3, depth, wide), f32),
         ),
         in_specs=[any_space] * 2,
-        out_specs=[any_space] * 3,
+        out_specs=[pl.BlockSpec(memory_space=pltpu.VMEM), any_space, any_space],
         scratch_shapes=[
             pltpu.VMEM((2, depth, wide), f32),
-            pltpu.VMEM((rows, wide), f32),
             pltpu.VMEM((rows, wide), f32),
             pltpu.VMEM((2, tall, half), f32),
             pltpu.VMEM((2, half, wide), f32),
@@ -578,9 +599,8 @@
             pltpu.SemaphoreType.DMA((copies,)),
             pltpu.SemaphoreType.DMA((2,)),
             pltpu.SemaphoreType.DMA((2,)),
-            pltpu.SemaphoreType.DMA((len(PARTS),)),
         ],
-        compiler_params=pltpu.CompilerParams(collective_id=0, has_side_effects=True, vmem_limit_bytes=67043328),
+        compiler_params=pltpu.CompilerParams(collective_id=0, has_side_effects=True, vmem_limit_bytes=56500000),
         name="line",
     )(left_factor, right_factor)[0]
 

time: 315 us -> 306 us (0.971)
  Pallas kernels: 308 us -> 299 us
    pallas_call x1, Pallas kernels: 308 us -> 299 us  [line(): pl.pallas_call(kernel, out_shape=(pltpu.VMEM((rows, wide), f32), jax.Shap...]
where the time goes in v1:
time: 306 us; the launch traced here: 301 us
  Pallas kernels  299 us (98%)
    pallas_call x1, Pallas kernels, line(): pl.pallas_call(kernel, out_shape=(pltpu.VMEM((rows, wide), f32), jax.Shap...  299 us

profile of v1, /device:TPU:15, one launch (start us, length us, event | category | flops | bytes accessed | tf_op | source)
XLA Modules:
  0.0 301.0 jit_solution(1169097887147468209)
XLA Ops:
  0.0 298.8 %line.1 = (f32[768,1536]{1,0:T(8,128)S(1)}, f32[3,768,2048]{2,1,0:T(8,128)}, f32[3,2048,1536]{2,1,0:T(8,128)}) custom-call(f32[1536,2048]{1,0:T(8,128)} %left.1, f32[2048,1536]{1,0:T(8,128)} %right.1), custom_call_target="tpu_custom_call" | custom-call | tf_op jit(solution)/shard_map/line/pallas_call | solution.py:583
  298.8 2.2 copy.4

commit v2 on v1

--- a/solution.py
+++ b/solution.py
@@ -7,8 +7,8 @@
 
 MESH = pl.DeviceIdType.MESH
 EVEN = (1, 1, 1, 1)
-PARTS = (4, 4, 4, 2, 2)
-OUTER = ((0, None), (1, None), (2, 0), (2, 1), (3, None), (4, 0), (4, 1))
+PARTS = (4, 4, 2, 2, 2, 2)
+OUTER = ((0, None), (1, None), (2, None), (3, None), (4, None), (5, 0), (5, 1))
 LANES = 512
 LAST = 3
 PIECES = 8
@@ -190,20 +190,20 @@
         runs, first = [], []
         for kind, *what in plan:
             if kind == "run":
-                runs.append((what, [], []))
+                runs.append((what, [], [], []))
             elif not runs:
                 first.append(what[0])
             else:
-                runs[-1][1 if kind == "do" else 2].append(what[0])
+                runs[-1][("do", "then", "gap").index(kind) + 1].append(what[0])
         for act in first:
             act()
         base = 0
-        for index, ((count, load, use), acts, after) in enumerate(runs):
+        for index, ((count, load, use), acts, after, gap) in enumerate(runs):
             if index == 0:
                 load(0, 0)
             following = runs[index + 1][0][1] if index + 1 < len(runs) else None
 
-            def step(j, carry, count=count, load=load, use=use, acts=acts, following=following, base=base):
+            def step(j, carry, count=count, load=load, use=use, acts=acts, following=None if gap else following, base=base):
                 slot = lax.rem(j + base, 2)
 
                 @pl.when(j + 1 < count)
@@ -221,9 +221,11 @@
                 return carry
 
             lax.fori_loop(0, count, step, 0)
-            for act in after:
+            base = (base + count) % 2
+            for act in after + gap:
                 act()
-            base = (base + count) % 2
+            if gap:
+                following(0, base)
 
     def own_jobs(count, job):
         def load(j, slot):
@@ -473,6 +475,9 @@
 
         def then(act, *args):
             plan.append(("then", lambda: act(*args)))
+
+        def gap(act, *args):
+            plan.append(("gap", lambda: act(*args)))
 
         def only(side, acts):
             def act():
@@ -540,31 +545,30 @@
         plan.append(far_units([outer_far], [0, 2], [0]))
         do(take_x, 6)
         do(outer_arrived, 2)
-        plan.append(outer_extra(2, (0,)))
-        do(ahead, 5)
-        plan.append(outer_units(2, (0,)))
-        do(ahead, 6)
-        do(outer_arrived, 3)
-        plan.append(outer_extra(2, (1,)))
+        plan.append(outer_extra(2))
         then(send_sum, 2)
-        plan.append(outer_units(2, (1,)))
+        for k in (5, 6):
+            gap(ahead, k)
+        gap(outer_arrived, 3)
+        plan.append(outer_extra(3))
+        then(send_sum, 3)
         do(take_x, 7)
+        plan.append(outer_units(2))
         do(take_y, 4)
         do(whole, 1)
-        plan.append(far_units([inner_far], [1], [0, 1]))
-        plan.append(far_units([outer_far], [1], [0]))
+        plan.append(far_list([(inner_far, 1, 0), (inner_far, 1, 1), (outer_far, 1, 0)]))
+        gap(take_y, 5)
+        gap(outer_arrived, 4)
+        plan.append(outer_extra(4))
+        then(send_sum, 4)
+        do(take_y, 6)
         plan.append(own_jobs(1, lambda j: (outer_far, layer * half, 2 * tall)))
-        do(take_y, 5)
-        do(outer_arrived, 4)
-        plan.append(outer_extra(3))
-        then(send_sum, 3)
-        do(take_y, 6)
-        do(outer_arrived, 5)
-        plan.append(outer_extra(4, (0,)))
+        gap(outer_arrived, 5)
+        plan.append(outer_extra(5, (0,)))
         plan.append(own_jobs(2, lambda j: (jnp.where(j == 0, outer_term, outer_far), layer * half, 3 * tall)))
         do(take_y, 7)
         do(outer_arrived, 6)
-        plan.append(outer_extra(4, (1,)))
+        plan.append(outer_extra(5, (1,)))
         do(whole, 3)
         plan.append(far_list([(inner_far, 3, 0), (inner_far, 3, 1), (outer_far, 3, 0), (outer_far, 2, 1), (outer_far, 3, 1)]))
         plan.append(outer_units(3, (1,)))

time: 306 us -> 303 us (level); the launches traced: 301 us -> 301 us
  no operation moved by 1% of the time
where the time goes in v2:
time: 303 us; the launch traced here: 301 us
  Pallas kernels  299 us (99%)
    pallas_call x1, Pallas kernels, line(): pl.pallas_call(kernel, out_shape=(pltpu.VMEM((rows, wide), f32), jax.Shap...  299 us

profile of v2, /device:TPU:15, one launch (start us, length us, event | category | flops | bytes accessed | tf_op | source)
XLA Modules:
  0.0 301.3 jit_solution(6744323481634822701)
XLA Ops:
  0.0 299.1 %line.1 = (f32[768,1536]{1,0:T(8,128)S(1)}, f32[3,768,2048]{2,1,0:T(8,128)}, f32[3,2048,1536]{2,1,0:T(8,128)}) custom-call(f32[1536,2048]{1,0:T(8,128)} %left.1, f32[2048,1536]{1,0:T(8,128)} %right.1), custom_call_target="tpu_custom_call" | custom-call | tf_op jit(solution)/shard_map/line/pallas_call | solution.py:587
  299.1 2.2 copy.4
